TPU v7x, 32 devices: a whole 2x2x4 slice. The times are simulated.
32 devices in a mesh: leaf: 32 (over z, y, x, core).
Axes of the slice: x: 2, y: 2, z: 4, core: 2. Of those that a mesh axis runs over, the one named last changes fastest.
Arguments:
- slip: bfloat16 [128, 8192], P(None, 'leaf'), may hold values from -6 to 6
- to_multipole: bfloat16 [121, 128], replicated, may hold values from -0.5 to 0.5
- up_shift: float32 [2, 121, 121], replicated, may hold values from -0.375 to 0.375
- down_shift: float32 [2, 121, 121], replicated, may hold values from -0.5 to 0.5
- sibling_far: float32 [2, 121, 121], replicated, may hold values from -0.5 to 0.5
- leaf_far: bfloat16 [27, 121, 121], replicated, may hold values from -0.25 to 0.25
- to_stress: bfloat16 [128, 121], replicated, may hold values from -0.125 to 0.125
- near_blocks: bfloat16 [9, 128, 128], replicated, may hold values from -0.1875 to 0.1875
- send_cells: int32 [32, 4096], P('leaf'), may hold values from 0 to 255, as said below
- far_list: int32 [27, 8192], P(None, 'leaf'), may hold values from 0 to 4351, as said below
- near_list: int32 [9, 8192], P(None, 'leaf'), may hold values from 0 to 319, as said below
Outputs:
- stress: float32 [128, 8192], P(None, 'leaf')
Inputs may be any that keep to these rules, and one draw needn't show every extreme that they name: `send_cells`: row q holds, in positions d * 128 to (d + 1) * 128 - 1, 128 distinct cells of device q (numbered within that device) listed for receiving device d. `far_list`: an entry v below 256 names a cell of the target's own device. Otherwise v - 256 = q * 128 + s names slot s of device q's list for the target's device, q is not the target's device, s < 128 when q lies within 4 devices of it and s < 32 when it lies farther; in every draw some entry names slot 127 of a device within 4, and some names slot 31 of a farther device. `near_list`: an entry w names the cell w - 32 counted from the first cell of the target's device, so that positions before 0 and from 256 on lie on the neighbouring devices (zeros outside the fault); entry 4 is the target itself.
All inputs are finite; a program needn't handle non-finite values.
Results may differ from a plain program's by a relative error of at most 0.0031.
Values may be sent and summed in bfloat16 or wider, within the bound.
A program may use at most 64 MiB of HBM per device.

v0:
```python
import jax
import jax.numpy as jnp
from jax import lax
from jax.sharding import PartitionSpec as P

NEAR = 9
TYPES = 27
HALO = 32


def with_halo(block, sides, width):
    for axis, dim in sides:
        count = lax.axis_size(axis)
        forward = [(i, i + 1) for i in range(count - 1)]
        backward = [(target, source) for source, target in forward]
        low = lax.ppermute(
            lax.slice_in_dim(block, block.shape[dim] - width, None, axis=dim), axis, forward
        )
        high = lax.ppermute(lax.slice_in_dim(block, 0, width, axis=dim), axis, backward)
        block = jnp.concatenate([low, block, high], axis=dim)
    return block


def swapped(block, axis, stride):
    count = lax.axis_size(axis)
    route = []
    for low in range(count):
        high = low | 1 << stride
        if high != low and high < count:
            route += [(low, high), (high, low)]
    return lax.ppermute(block, axis, route)


def pair_up(up_shift, lower, upper):
    precise = lax.Precision.HIGHEST
    return jnp.dot(up_shift[0], lower, precision=precise) + jnp.dot(
        up_shift[1], upper, precision=precise
    )


def body(
    slip,
    to_multipole,
    up_shift,
    down_shift,
    sibling_far,
    leaf_far,
    to_stress,
    near_blocks,
    send_cells,
    far_list,
    near_list,
):
    precise = lax.Precision.HIGHEST
    cells_here = slip.shape[1]
    coef_count = to_multipole.shape[0]
    devices_all = lax.axis_size("leaf")
    own_index = lax.axis_index("leaf")
    multipole = jnp.dot(to_multipole, slip, preferred_element_type=jnp.float32).astype(jnp.bfloat16)
    extended = with_halo(slip, (("leaf", 1),), HALO)
    near_cols = jnp.take(extended, near_list.reshape(-1), axis=1).reshape(
        extended.shape[0], NEAR, cells_here
    )
    near_part = jnp.einsum(
        "kij,jkc->ic", near_blocks, near_cols, preferred_element_type=jnp.float32
    )
    send_row = send_cells[0]
    outgoing = jnp.take(multipole, send_row, axis=1)
    arrived = lax.all_to_all(outgoing, "leaf", split_axis=1, concat_axis=1, tiled=True)
    sources = jnp.concatenate([multipole, arrived], axis=1)
    leaf_cols = jnp.take(sources, far_list.reshape(-1), axis=1).reshape(
        coef_count, TYPES, cells_here
    )
    leaf_sum = jnp.einsum("tij,jtc->ic", leaf_far, leaf_cols, preferred_element_type=jnp.float32)
    local_levels = cells_here.bit_length() - 1
    aggregates = [multipole.astype(jnp.float32)]
    for height in range(local_levels):
        below = aggregates[-1]
        aggregates.append(pair_up(up_shift, below[:, 0::2], below[:, 1::2]))
    root_sum = aggregates[-1]
    tree_bits = devices_all.bit_length() - 1
    siblings = []
    current = root_sum
    for tree_bit in range(tree_bits):
        partner = swapped(current, "leaf", tree_bit)
        siblings.append(partner)
        if tree_bit + 1 < tree_bits:
            branch = own_index >> tree_bit & 1
            lower = jnp.where(branch == 0, current, partner)
            upper = jnp.where(branch == 0, partner, current)
            current = pair_up(up_shift, lower, upper)
    expansion = jnp.zeros((coef_count, 1), jnp.float32)
    for tree_bit in reversed(range(tree_bits)):
        branch = own_index >> tree_bit & 1
        down_pick = lax.dynamic_index_in_dim(down_shift, branch, 0, keepdims=False)
        far_pick = lax.dynamic_index_in_dim(sibling_far, branch, 0, keepdims=False)
        expansion = jnp.dot(down_pick, expansion, precision=precise) + jnp.dot(
            far_pick, siblings[tree_bit], precision=precise
        )
    for height in reversed(range(local_levels)):
        left_part = jnp.dot(down_shift[0], expansion, precision=precise)
        right_part = jnp.dot(down_shift[1], expansion, precision=precise)
        if height >= 1:
            level_sums = aggregates[height]
            left_part = left_part + jnp.dot(sibling_far[0], level_sums[:, 1::2], precision=precise)
            right_part = right_part + jnp.dot(
                sibling_far[1], level_sums[:, 0::2], precision=precise
            )
        expansion = jnp.stack([left_part, right_part], axis=-1).reshape(coef_count, -1)
    local_exp = (expansion + leaf_sum).astype(jnp.bfloat16)
    return jnp.dot(to_stress, local_exp, preferred_element_type=jnp.float32) + near_part


def solution(mesh):
    return jax.shard_map(
        body,
        mesh=mesh,
        in_specs=(
            P(None, "leaf"),
            P(),
            P(),
            P(),
            P(),
            P(),
            P(),
            P(),
            P("leaf", None),
            P(None, "leaf"),
            P(None, "leaf"),
        ),
        out_specs=P(None, "leaf"),
        check_vma=False,
    )
```

profile of v0, /device:TPU:0, one launch (start us, length us, event | category | flops | bytes accessed | tf_op | source)
XLA Modules:
  0.0 93.2 jit_solution(9481325740652045898)
XLA Ops:
  0.0 1.1 %convolution_convert_fusion = bf16[121,256]{1,0:T(8,128)(2,1)S(1)} fusion(bf16[121,128]{1,0:T(8,128)(2,1)} %param.12, bf16[128,256]{1,0:T(8,128)(2,1)} %param.11), kind=kOutput, calls=%fused_computation.12 | convolution fusion | flops 7960832 | bytes 158464 | tf_op jit(solution)/shard_map/dot_general | solution.py:59
  1.1 1.2 %slice.50 = bf16[121,128]{1,0:T(8,128)(2,1)S(1)} slice(bf16[121,256]{1,0:T(8,128)(2,1)S(1)} %convolution_convert_fusion), slice={[0:121:1], [0:256:2]} | slice | bytes 61952 | tf_op jit(solution)/shard_map/slice | solution.py:79
  2.3 1.2 %slice.52 = bf16[121,128]{1,0:T(8,128)(2,1)S(1)} slice(bf16[121,256]{1,0:T(8,128)(2,1)S(1)} %convolution_convert_fusion), slice={[0:121:1], [1:256:2]} | slice | bytes 61952 | tf_op jit(solution)/shard_map/slice | solution.py:79
  3.4 1.1 %fusion.97 = (f32[1,121,121]{2,0,1:T(1,128)S(1)}, f32[1,121,121]{2,0,1:T(1,128)S(1)}) fusion(f32[2,121,121]{2,0,1:T(2,128)} %param.13), kind=kLoop, calls=%fused_computation.195 | loop fusion | bytes 234256 | tf_op jit(solution)/shard_map/slice | solution.py:36
  8.2 0.8 fusion.57
  8.9 0.5 collective-permute-start
  9.6 12.1 %gather_fusion = bf16[4096,121]{1,0:T(8,128)(2,1)S(1)} fusion(bf16[121,256]{0,1:T(8,128)(2,1)S(1)} %copy.42, s32[4096]{0:T(1024)S(1)} %broadcast_clamp_fusion), kind=kCustom, calls=%fused_computation | custom fusion | bytes 1998848 | tf_op jit(solution)/shard_map/jit(_take)/gather | solution.py:68
  21.8 1.5 %broadcast_select_fusion = bf16[121,32,128]{0,2,1:T(8,128)(2,1)} fusion(bf16[121,32,128]{0,2,1:T(8,128)(2,1)S(1)} %bitcast.403, pred[32,128]{1,0:T(8,128)(4,1)S(1)} %compare_and_fusion.2), kind=kLoop, calls=%fused_computation.102 | loop fusion | flops 495616 | bytes 1986560 | tf_op jit(solution)/shard_map/jit(_take)/select_n | solution.py:68
  23.3 7.0 %all-to-all-start = ((bf16[121,32,128]{0,2,1:T(8,128)(2,1)}), bf16[121,32,128]{0,2,1:T(8,128)(2,1)S(1)}, u32[]{:S(2)}, u32[]{:S(2)}) async-start(bf16[121,32,128]{0,2,1:T(8,128)(2,1)} %broadcast_select_fusion), calls=%async_computation | async-start | bytes 2097152 | tf_op jit(solution)/shard_map/all_to_all | solution.py:69
  30.4 0.6 fusion.98
  31.0 2.7 %collective-permute-start.5 = (bf16[128,32]{0,1:T(8,128)(2,1)}, bf16[128,32]{0,1:T(8,128)(2,1)}, u32[]{:S(2)}, u32[]{:S(2)}) collective-permute-start(bf16[128,32]{0,1:T(8,128)(2,1)} %get-tuple-element.21), channel_id=1, source_target_pairs={{0,1},{1,2},{2,3},{3,4},{4,5},{5,6},{6,7},{7,8},{8,9},{9,10},{10,1... | collective-permute-start | bytes 24584 | tf_op jit(solution)/shard_map/ppermute | solution.py:16
  33.8 1.5 %collective-permute-start.6 = (bf16[128,32]{0,1:T(8,128)(2,1)}, bf16[128,32]{0,1:T(8,128)(2,1)}, u32[]{:S(2)}, u32[]{:S(2)}) collective-permute-start(bf16[128,32]{0,1:T(8,128)(2,1)} %get-tuple-element.22), channel_id=1, source_target_pairs={{1,0},{2,1},{3,2},{4,3},{5,4},{6,5},{7,6},{8,7},{9,8},{10,9},{11,1... | collective-permute-start | bytes 24584 | tf_op jit(solution)/shard_map/ppermute | solution.py:19
  35.3 0.6 compare_and_fusion
  35.9 0.6 compare_and_fusion.1
  36.5 0.8 fusion.95
  37.4 0.8 convolution_bitcast_fusion.22
  38.3 0.8 fusion.55
  39.1 3.4 %collective-permute-start.1 = (f32[121,1]{0,1:T(1,128)S(1)}, f32[121,1]{0,1:T(1,128)S(1)}, u32[]{:S(2)}, u32[]{:S(2)}) collective-permute-start(f32[121,1]{0,1:T(1,128)S(1)} %fusion.55), channel_id=1, source_target_pairs={{0,2},{2,0},{1,3},{3,1},{4,6},{6,4},{5,7},{7,5},{8,10},{10,8},{9,1... | collective-permute-start | bytes 1460 | tf_op jit(solution)/shard_map/ppermute | solution.py:31
  42.7 1.3 %collective-permute-done.1 = f32[121,1]{0,1:T(1,128)S(1)} collective-permute-done((f32[121,1]{0,1:T(1,128)S(1)}, f32[121,1]{0,1:T(1,128)S(1)}, u32[]{:S(2)}, u32[]{:S(2)}) %collective-permute-start.1) | collective-permute-done | bytes 516 | tf_op jit(solution)/shard_map/ppermute | solution.py:31
  44.4 3.0 %collective-permute-start.2 = (f32[121,1]{0,1:T(1,128)S(1)}, f32[121,1]{0,1:T(1,128)S(1)}, u32[]{:S(2)}, u32[]{:S(2)}) collective-permute-start(f32[121,1]{0,1:T(1,128)S(1)} %fusion.53), channel_id=1, source_target_pairs={{0,4},{4,0},{1,5},{5,1},{2,6},{6,2},{3,7},{7,3},{8,12},{12,8},{9,1... | collective-permute-start | bytes 1460 | tf_op jit(solution)/shard_map/ppermute | solution.py:31
  47.4 1.5 %collective-permute-done.2 = f32[121,1]{0,1:T(1,128)S(1)} collective-permute-done((f32[121,1]{0,1:T(1,128)S(1)}, f32[121,1]{0,1:T(1,128)S(1)}, u32[]{:S(2)}, u32[]{:S(2)}) %collective-permute-start.2) | collective-permute-done | bytes 516 | tf_op jit(solution)/shard_map/ppermute | solution.py:31
  49.3 3.0 %collective-permute-start.3 = (f32[121,1]{0,1:T(1,128)S(1)}, f32[121,1]{0,1:T(1,128)S(1)}, u32[]{:S(2)}, u32[]{:S(2)}) collective-permute-start(f32[121,1]{0,1:T(1,128)S(1)} %fusion.51), channel_id=1, source_target_pairs={{0,8},{8,0},{1,9},{9,1},{2,10},{10,2},{3,11},{11,3},{4,12},{12,4},... | collective-permute-start | bytes 1460 | tf_op jit(solution)/shard_map/ppermute | solution.py:31
  52.3 1.5 %collective-permute-done.3 = f32[121,1]{0,1:T(1,128)S(1)} collective-permute-done((f32[121,1]{0,1:T(1,128)S(1)}, f32[121,1]{0,1:T(1,128)S(1)}, u32[]{:S(2)}, u32[]{:S(2)}) %collective-permute-start.3) | collective-permute-done | bytes 516 | tf_op jit(solution)/shard_map/ppermute | solution.py:31
  54.3 3.0 %collective-permute-start.4 = (f32[121,1]{0,1:T(1,128)S(1)}, f32[121,1]{0,1:T(1,128)S(1)}, u32[]{:S(2)}, u32[]{:S(2)}) collective-permute-start(f32[121,1]{0,1:T(1,128)S(1)} %fusion.49), channel_id=1, source_target_pairs={{0,16},{16,0},{1,17},{17,1},{2,18},{18,2},{3,19},{19,3},{4,20},{20... | collective-permute-start | bytes 1460 | tf_op jit(solution)/shard_map/ppermute | solution.py:31
  57.3 1.5 %collective-permute-done.4 = f32[121,1]{0,1:T(1,128)S(1)} collective-permute-done((f32[121,1]{0,1:T(1,128)S(1)}, f32[121,1]{0,1:T(1,128)S(1)}, u32[]{:S(2)}, u32[]{:S(2)}) %collective-permute-start.4) | collective-permute-done | bytes 516 | tf_op jit(solution)/shard_map/ppermute | solution.py:31
  60.6 0.9 fusion.39
  68.8 0.7 pad_maximum_fusion.2
  69.6 4.7 %gather_fusion.2 = bf16[2304,128]{1,0:T(8,128)(2,1)S(1)} fusion(bf16[128,320]{0,1:T(8,128)(2,1)S(1)} %pad_maximum_fusion.2, s32[3072]{0:T(1024)S(1)} %pad_clamp_fusion.1), kind=kCustom, calls=%fused_computation.2 | custom fusion | bytes 1188864 | tf_op jit(solution)/shard_map/jit(_take)/gather | solution.py:61
  74.3 0.5 convolution_bitcast_fusion
  75.0 14.7 %gather_fusion.1 = bf16[6912,121]{1,0:T(8,128)(2,1)} fusion(bf16[121,4352]{0,1:T(8,128)(2,1)S(1)} %pad_maximum_fusion, s32[7168]{0:T(1024)S(1)} %pad_clamp_fusion), kind=kCustom, calls=%fused_computation.1 | custom fusion | bytes 3373056 | tf_op jit(solution)/shard_map/jit(_take)/gather | solution.py:71
  89.8 2.7 %fusion.6 = f32[128,256]{0,1:T(8,128)S(1)} fusion(f32[256,128]{1,0:T(8,128)S(1)} %convolution_bitcast_fusion, bf16[128,121]{1,0:T(8,128)(2,1)S(1)} %copy-done.10, f32[121,256]{0,1:T(8,128)S(1)} %bitcast.413, bf16[27,121,121]{2,1,0:T(8,128)(2,1)S(1)} %copy-done, bf16[121,27,256]{0,2,1:T(8,128)(2,1)} %bitcast.405, pred[27,256]{1,0:T(8,128)(4,1)S(1)} %copy-done.7), kind=kOutput, calls=%fused_computation.9 | convolution fusion | flops 211258112 | bytes 2887254 | tf_op jit(solution)/shard_map/dot_general | solution.py:111
  92.4 0.8 copy.46
  (124 shorter events, 14.5 us)
Async XLA Ops:
  0.0 89.7 %copy-start = (bf16[27,121,121]{2,1,0:T(8,128)(2,1)S(1)}, bf16[27,121,121]{2,1,0:T(8,128)(2,1)}, u32[]{:S(2)}) copy-start(bf16[27,121,121]{2,1,0:T(8,128)(2,1)} %param.16) | copy-start | bytes 2371846
  0.0 9.5 %copy-start.5 = (s32[1,4096]{1,0:T(1,128)S(1)}, s32[1,4096]{1,0:T(1,128)}, u32[]{:S(2)}) copy-start(s32[1,4096]{1,0:T(1,128)} %param.19) | copy-start | bytes 49156
  8.9 28.5 %collective-permute-start = (f32[121,1]{0,1:T(1,128)}, f32[121,1]{0,1:T(1,128)}, u32[]{:S(2)}, u32[]{:S(2)}) collective-permute-start(f32[121,1]{0,1:T(1,128)} %fusion.57), channel_id=1, source_target_pairs={{0,1},{1,0},{2,3},{3,2},{4,5},{5,4},{6,7},{7,6},{8,9},{9,8},{10,11... | collective-permute-start | bytes 1460 | tf_op jit(solution)/shard_map/ppermute | solution.py:31
  21.7 8.5 %copy-start.3 = (bf16[128,256]{1,0:T(8,128)(2,1)S(1)}, bf16[128,256]{1,0:T(8,128)(2,1)}, u32[]{:S(2)}) copy-start(bf16[128,256]{1,0:T(8,128)(2,1)} %param.11) | copy-start | bytes 196612
  21.8 13.5 %copy-start.4 = (s32[27,256]{1,0:T(8,128)S(1)}, s32[27,256]{1,0:T(8,128)}, u32[]{:S(2)}) copy-start(s32[27,256]{1,0:T(8,128)} %param.20) | copy-start | bytes 82948
  21.8 14.1 %copy-start.6 = (s32[9,256]{1,0:T(8,128)S(1)}, s32[9,256]{1,0:T(8,128)}, u32[]{:S(2)}) copy-start(s32[9,256]{1,0:T(8,128)} %param.21) | copy-start | bytes 27652
  21.8 14.7 %copy-start.1 = (f32[2,121,121]{2,0,1:T(2,128)S(1)}, f32[2,121,121]{2,0,1:T(2,128)}, u32[]{:S(2)}) copy-start(f32[2,121,121]{2,0,1:T(2,128)} %param.15) | copy-start | bytes 351388
  21.8 14.7 %copy-start.2 = (f32[2,121,121]{2,0,1:T(2,128)S(1)}, f32[2,121,121]{2,0,1:T(2,128)}, u32[]{:S(2)}) copy-start(f32[2,121,121]{2,0,1:T(2,128)} %param.14) | copy-start | bytes 351388
  23.3 51.4 %all-to-all-start = ((bf16[121,32,128]{0,2,1:T(8,128)(2,1)}), bf16[121,32,128]{0,2,1:T(8,128)(2,1)S(1)}, u32[]{:S(2)}, u32[]{:S(2)}) async-start(bf16[121,32,128]{0,2,1:T(8,128)(2,1)} %broadcast_select_fusion), calls=%async_computation | async-start | bytes 2097152 | tf_op jit(solution)/shard_map/all_to_all | solution.py:69
  31.0 37.8 %collective-permute-start.5 = (bf16[128,32]{0,1:T(8,128)(2,1)}, bf16[128,32]{0,1:T(8,128)(2,1)}, u32[]{:S(2)}, u32[]{:S(2)}) collective-permute-start(bf16[128,32]{0,1:T(8,128)(2,1)} %get-tuple-element.21), channel_id=1, source_target_pairs={{0,1},{1,2},{2,3},{3,4},{4,5},{5,6},{6,7},{7,8},{8,9},{9,10},{10,1... | collective-permute-start | bytes 24584 | tf_op jit(solution)/shard_map/ppermute | solution.py:16
  33.8 35.1 %collective-permute-start.6 = (bf16[128,32]{0,1:T(8,128)(2,1)}, bf16[128,32]{0,1:T(8,128)(2,1)}, u32[]{:S(2)}, u32[]{:S(2)}) collective-permute-start(bf16[128,32]{0,1:T(8,128)(2,1)} %get-tuple-element.22), channel_id=1, source_target_pairs={{1,0},{2,1},{3,2},{4,3},{5,4},{6,5},{7,6},{8,7},{9,8},{10,9},{11,1... | collective-permute-start | bytes 24584 | tf_op jit(solution)/shard_map/ppermute | solution.py:19
  39.1 4.9 %collective-permute-start.1 = (f32[121,1]{0,1:T(1,128)S(1)}, f32[121,1]{0,1:T(1,128)S(1)}, u32[]{:S(2)}, u32[]{:S(2)}) collective-permute-start(f32[121,1]{0,1:T(1,128)S(1)} %fusion.55), channel_id=1, source_target_pairs={{0,2},{2,0},{1,3},{3,1},{4,6},{6,4},{5,7},{7,5},{8,10},{10,8},{9,1... | collective-permute-start | bytes 1460 | tf_op jit(solution)/shard_map/ppermute | solution.py:31
  44.4 4.5 %collective-permute-start.2 = (f32[121,1]{0,1:T(1,128)S(1)}, f32[121,1]{0,1:T(1,128)S(1)}, u32[]{:S(2)}, u32[]{:S(2)}) collective-permute-start(f32[121,1]{0,1:T(1,128)S(1)} %fusion.53), channel_id=1, source_target_pairs={{0,4},{4,0},{1,5},{5,1},{2,6},{6,2},{3,7},{7,3},{8,12},{12,8},{9,1... | collective-permute-start | bytes 1460 | tf_op jit(solution)/shard_map/ppermute | solution.py:31
  49.3 4.6 %collective-permute-start.3 = (f32[121,1]{0,1:T(1,128)S(1)}, f32[121,1]{0,1:T(1,128)S(1)}, u32[]{:S(2)}, u32[]{:S(2)}) collective-permute-start(f32[121,1]{0,1:T(1,128)S(1)} %fusion.51), channel_id=1, source_target_pairs={{0,8},{8,0},{1,9},{9,1},{2,10},{10,2},{3,11},{11,3},{4,12},{12,4},... | collective-permute-start | bytes 1460 | tf_op jit(solution)/shard_map/ppermute | solution.py:31
  54.3 4.6 %collective-permute-start.4 = (f32[121,1]{0,1:T(1,128)S(1)}, f32[121,1]{0,1:T(1,128)S(1)}, u32[]{:S(2)}, u32[]{:S(2)}) collective-permute-start(f32[121,1]{0,1:T(1,128)S(1)} %fusion.49), channel_id=1, source_target_pairs={{0,16},{16,0},{1,17},{17,1},{2,18},{18,2},{3,19},{19,3},{4,20},{20... | collective-permute-start | bytes 1460 | tf_op jit(solution)/shard_map/ppermute | solution.py:31
  69.5 4.7 %copy-start.8 = (pred[9,256]{1,0:T(8,128)(4,1)S(1)}, pred[9,256]{1,0:T(8,128)(4,1)}, u32[]{:S(2)}) copy-start(pred[9,256]{1,0:T(8,128)(4,1)} %compare_and_fusion.1) | copy-start | bytes 6916
  69.6 4.7 %copy-start.9 = (bf16[9,128,128]{2,1,0:T(8,128)(2,1)S(1)}, bf16[9,128,128]{2,1,0:T(8,128)(2,1)}, u32[]{:S(2)}) copy-start(bf16[9,128,128]{2,1,0:T(8,128)(2,1)} %param.18) | copy-start | bytes 884740
  75.0 14.7 %copy-start.7 = (pred[27,256]{1,0:T(8,128)(4,1)S(1)}, pred[27,256]{1,0:T(8,128)(4,1)}, u32[]{:S(2)}) copy-start(pred[27,256]{1,0:T(8,128)(4,1)} %compare_and_fusion) | copy-start | bytes 20740
  75.0 14.7 %copy-start.10 = (bf16[128,121]{1,0:T(8,128)(2,1)S(1)}, bf16[128,121]{1,0:T(8,128)(2,1)}, u32[]{:S(2)}) copy-start(bf16[128,121]{1,0:T(8,128)(2,1)} %param.17) | copy-start | bytes 92932
where the time goes:
time: 93.6 us; the launch traced here: 93.2 us
  local copies, waits for them, and re-layouts  38 us (41%)
  starting transfers between devices  24 us (26%)
  matrix products  20.6 us (22%)
  waiting for transfers between devices  5.89 us (6%)
  other arithmetic  3.99 us (4%)
    gather x1, local copies, waits for them, and re-layouts, body(): jnp.take(sources, far_list.reshape(-1), axis=1)  14.7 us
    ppermute x5, starting transfers between devices, swapped(): return lax.ppermute(block, axis, route)  12.9 us
    gather x1, local copies, waits for them, and re-layouts, body(): outgoing = jnp.take(multipole, send_row, axis=1)  12.1 us
    all_to_all x1, starting transfers between devices, body(): lax.all_to_all(outgoing, 'leaf', split_axis=1, concat_axis=1, tiled=True)  6.95 us
    ppermute x5, waiting for transfers between devices, swapped(): return lax.ppermute(block, axis, route)  5.89 us
    gather x1, local copies, waits for them, and re-layouts, body(): jnp.take(extended, near_list.reshape(-1), axis=1)  4.67 us
    dot_general x12, matrix products, pair_up(): jnp.dot(up_shift[1], upper, precision=precise)  3.71 us
    dot_general x12, matrix products, pair_up(): jnp.dot(up_shift[0], lower, precision=precise)  3.1 us
  transfers between devices with their start and end apart: 8, of which 4 were waited for; matrix products, arithmetic and copies ran while one was open for 38% of the time, Pallas kernels for 0%

commit v1 on v0

v1 whole, which is shorter than its diff:
```python
import functools

import jax
import jax.numpy as jnp
from jax import lax
from jax.experimental import pallas as pl
from jax.experimental.pallas import tpu as pltpu
from jax.sharding import PartitionSpec as P

HALO = 32
PEERS = 4
CAP_FAR = 32
LANES = 128
BF = jnp.bfloat16
F32 = jnp.float32
MESH = pl.DeviceIdType.MESH
OFFSETS = tuple(range(-PEERS, 0)) + tuple(range(1, PEERS + 1))


def mm(a, b):
    return jnp.dot(a, b, preferred_element_type=F32)


def halves(x):
    high = x.astype(BF)
    return high, (x - high.astype(F32)).astype(BF)


def one_hot(rows, index):
    count = index.shape[1]
    lines = lax.broadcasted_iota(jnp.int32, (rows, count), 0).astype(F32).astype(BF)
    hit = lines == jnp.broadcast_to(index.astype(BF), (rows, count))
    return jnp.where(hit, jnp.ones((), BF), jnp.zeros((), BF))


def kernel(
    n, cells, cap,
    slip_ref, tm_ref, up_ref, down_ref, sib_ref, leaf_ref, ts_ref, nb_ref, send_ref, far_ref, near_ref,
    out_ref,
    outgoing, far_buf, near_buf, edges, halo, root_out, roots,
    weight, w_up, w_sib, w_down, agg, terms, loc, rel, near_rel, source,
    far_send, far_recv, near_send, near_recv, halo_send, halo_recv, root_send, root_recv,
):
    me = lax.axis_index("leaf")
    coef = tm_ref.shape[0]
    types = far_ref.shape[0]
    kinds = near_ref.shape[0]
    rest = cap - CAP_FAR

    barrier = pltpu.get_barrier_semaphore()

    far_buf[...] = jnp.zeros_like(far_buf)
    near_buf[...] = jnp.zeros_like(near_buf)
    halo[...] = jnp.zeros_like(halo)

    def greet(k, carry):
        pl.semaphore_signal(barrier, inc=1, device_id=(lax.rem(me + k, n),), device_id_type=MESH)
        return carry

    lax.fori_loop(1, n, greet, 0)

    edges[0] = slip_ref[:, :LANES].astype(F32).T[:HALO].astype(BF)
    edges[1] = slip_ref[:, cells - LANES :].astype(F32).T[LANES - HALO :].astype(BF)

    weight[...] = jnp.zeros_like(weight)
    weight[0, :coef, :] = tm_ref[...].astype(F32)
    multipole = mm(weight[0].astype(BF), slip_ref[...]).astype(BF)
    source[:, :cells] = multipole

    chunk = 4 * cap
    for start in range(0, n * cap, chunk):
        picked = one_hot(cells, send_ref[0:1, start : start + chunk].astype(F32))
        outgoing[start : start + chunk, :] = mm(multipole, picked).T.astype(BF)

    pl.semaphore_wait(barrier, n - 1)

    def far_copy(k):
        target = lax.rem(me + k, n)
        return pltpu.make_async_remote_copy(
            src_ref=outgoing.at[pl.ds(pl.multiple_of(target * cap, cap), CAP_FAR)],
            dst_ref=far_buf.at[pl.ds(pl.multiple_of(me * CAP_FAR, CAP_FAR), CAP_FAR)],
            send_sem=far_send.at[k],
            recv_sem=far_recv.at[k],
            device_id=(target,),
            device_id_type=MESH,
        )

    def near_copy(j):
        target = jnp.clip(me + OFFSETS[j], 0, n - 1)
        back = len(OFFSETS) - 1 - j
        return pltpu.make_async_remote_copy(
            src_ref=outgoing.at[pl.ds(pl.multiple_of(target * cap + CAP_FAR, CAP_FAR), rest)],
            dst_ref=near_buf.at[pl.ds(back * rest, rest)],
            send_sem=near_send.at[j],
            recv_sem=near_recv.at[back],
            device_id=(target,),
            device_id_type=MESH,
        )

    def halo_copy(side):
        target = jnp.clip(me + (1 if side else -1), 0, n - 1)
        return pltpu.make_async_remote_copy(
            src_ref=edges.at[side],
            dst_ref=halo.at[pl.ds((1 - side) * HALO, HALO)],
            send_sem=halo_send.at[side],
            recv_sem=halo_recv.at[1 - side],
            device_id=(target,),
            device_id_type=MESH,
        )

    def root_copy(k):
        return pltpu.make_async_remote_copy(
            src_ref=root_out,
            dst_ref=roots.at[pl.ds(pl.multiple_of(me * 8, 8), 8)],
            send_sem=root_send.at[k],
            recv_sem=root_recv.at[k],
            device_id=(lax.rem(me + k, n),),
            device_id_type=MESH,
        )

    def inside(offset):
        return jnp.logical_and(me + offset >= 0, me + offset < n)

    for side in (0, 1):
        @pl.when(inside(1 if side else -1))
        def _():
            halo_copy(side).start()

    def start_far(k, carry):
        far_copy(k).start()
        return carry

    lax.fori_loop(1, n, start_far, 0)
    for j, offset in enumerate(OFFSETS):
        @pl.when(inside(offset))
        def _():
            near_copy(j).start()

    def parts(ref, index):
        weight[index, :coef, :coef] = ref
        weight[index, :coef, coef:] = jnp.zeros((coef, LANES - coef), F32)
        return halves(weight[index].T)

    w_sib[...] = jnp.zeros_like(w_sib)
    for s in (0, 1):
        high, low = parts(up_ref[s], 0 + s)
        w_up[s * LANES : (s + 1) * LANES, :LANES] = high
        w_up[s * LANES : (s + 1) * LANES, LANES:] = low
        high, low = parts(down_ref[s], 2 + s)
        w_down[:LANES, s * LANES : (s + 1) * LANES] = high
        w_down[LANES:, s * LANES : (s + 1) * LANES] = low
        high, low = parts(sib_ref[s], 4 + s)
        other = 1 - s
        w_sib[0, other * LANES : (other + 1) * LANES, s * LANES : (s + 1) * LANES] = high
        w_sib[1, other * LANES : (other + 1) * LANES, s * LANES : (s + 1) * LANES] = low

    def pair(base, rows):
        m = max(rows // 2, 8)
        even = agg[pl.ds(base, m, stride=2), :]
        odd = agg[pl.ds(base + 1, m, stride=2), :]
        return m, halves(jnp.concatenate([even, odd], axis=1))

    def lift(high, low):
        first = mm(high, w_up[...])
        second = mm(low, w_up[:, :LANES])
        return first[:, :LANES] + first[:, LANES:] + second

    def across(high, low):
        return mm(high, w_sib[0]) + mm(high, w_sib[1]) + mm(low, w_sib[0])

    def place(base, value):
        agg[base : base + value.shape[0], :] = value
        if value.shape[0] < 16:
            agg[base + value.shape[0] : base + 16, :] = jnp.zeros((16 - value.shape[0], LANES), F32)

    local_levels = cells.bit_length() - 1
    tree_bits = n.bit_length() - 1
    base, spot = 0, 0
    agg[:cells, :] = multipole.astype(F32).T
    local_spots = []
    for height in range(local_levels):
        rows = cells >> height
        m, (high, low) = pair(base, rows)
        if height >= 1:
            terms[spot : spot + m, :] = across(high, low)
            local_spots.append(spot)
            spot += m
        else:
            local_spots.append(None)
        value = lift(high, low)
        base += max(rows, 16)
        place(base, value)
    root_out[...] = value
    roots[pl.ds(pl.multiple_of(me * 8, 8), 8), :] = value

    def start_root(k, carry):
        root_copy(k).start()
        return carry

    lax.fori_loop(1, n, start_root, 0)

    v = far_ref[...]
    behind = v - cells
    sender = behind // cap
    slot = behind % cap
    delta = sender - me
    lane = jnp.where(delta < 0, delta + PEERS, delta + PEERS - 1)
    position = jnp.where(
        v < cells,
        v,
        jnp.where(
            slot < CAP_FAR,
            cells + sender * CAP_FAR + slot,
            cells + n * CAP_FAR + lane * rest + slot - CAP_FAR,
        ),
    )
    total = source.shape[1]
    blocks = total // 256
    for b in range(blocks):
        rel[b, :types, :] = jnp.clip(position - 256 * b, -1, 256).astype(F32)

    for side in (0, 1):
        @pl.when(inside(1 if side else -1))
        def _():
            halo_copy(side).wait_send()

        @pl.when(inside(-1 if side else 1))
        def _():
            halo_copy(side).wait_recv()

    w = near_ref[...]
    near_rel[0, :kinds, :] = jnp.clip(w - HALO, -1, cells).astype(F32)
    near_rel[1, :kinds, :] = jnp.where(
        w < HALO, w, jnp.where(w >= HALO + cells, w - cells, -1)
    ).astype(F32)
    slips = slip_ref[...]
    side_slips = jnp.concatenate(
        [halo[...], jnp.zeros((LANES - 2 * HALO, LANES), BF)], axis=0
    ).astype(F32).T.astype(BF)
    stress = jnp.zeros(out_ref.shape, F32)
    for k in range(kinds):
        column = mm(slips, one_hot(cells, near_rel[0, k : k + 1, :])) + mm(
            side_slips, one_hot(LANES, near_rel[1, k : k + 1, :])
        )
        stress = stress + mm(nb_ref[k], column.astype(BF))
    out_ref[...] = stress

    def wait_root(k, carry):
        root_copy(k).wait()
        return carry

    lax.fori_loop(1, n, wait_root, 0)
    base = 0
    place(base, roots[pl.ds(0, n, stride=8), :])
    tree_spots = []
    for bit in range(tree_bits):
        rows = n >> bit
        m, (high, low) = pair(base, rows)
        terms[spot : spot + m, :] = across(high, low)
        tree_spots.append(spot)
        spot += m
        if bit + 1 < tree_bits:
            value = lift(high, low)
            base += max(rows, 16)
            place(base, value)

    def descend(x):
        high, low = halves(x)
        return mm(high, w_down[:LANES, :]) + mm(high, w_down[LANES:, :]) + mm(low, w_down[:LANES, :])

    expansion = jnp.zeros((8, LANES), F32)
    for bit in reversed(range(tree_bits)):
        both = terms[pl.ds(tree_spots[bit] + (me >> (bit + 1)), 1), :]
        both = jnp.broadcast_to(both, (8, 2 * LANES))
        if bit + 1 < tree_bits:
            both = both + descend(expansion)
        expansion = jnp.where((me >> bit) & 1 == 0, both[:, :LANES], both[:, LANES:])
    for height in reversed(range(local_levels)):
        m = max((cells >> height) // 2, 8)
        both = descend(expansion)
        if height >= 1:
            both = both + terms[local_spots[height] : local_spots[height] + m, :]
        loc[pl.ds(0, m, stride=2), :] = both[:, :LANES]
        loc[pl.ds(1, m, stride=2), :] = both[:, LANES:]
        expansion = loc[: max(cells >> height, 8), :]

    def wait_far(k, carry):
        far_copy(k).wait()
        return carry

    lax.fori_loop(1, n, wait_far, 0)
    for j, offset in enumerate(OFFSETS):
        @pl.when(inside(offset))
        def _():
            near_copy(j).wait_send()

        @pl.when(inside(OFFSETS[len(OFFSETS) - 1 - j]))
        def _():
            near_copy(j).wait_recv()

    far_end = cells + n * CAP_FAR
    source[:, cells:far_end] = far_buf[...].astype(F32).T.astype(BF)
    source[:, far_end:] = near_buf[...].astype(F32).T.astype(BF)

    def leaf(t, acc):
        hits = jnp.concatenate(
            [one_hot(256, rel[b, pl.ds(t, 1), :]) for b in range(blocks)], axis=0
        )
        column = mm(source[...], hits).astype(BF)
        return acc + mm(leaf_ref[t], column[:coef])

    leaf_sum = lax.fori_loop(0, types, leaf, jnp.zeros((coef, cells), F32))
    local_exp = (expansion.T[:coef] + leaf_sum).astype(BF)
    out_ref[...] = out_ref[...] + mm(ts_ref[...], local_exp)


def round_up(value, unit):
    return -(-value // unit) * unit


def body(*args):
    slip, to_multipole, _, _, _, _, _, _, send_cells, far_list, near_list = args
    n = lax.axis_size("leaf")
    cells = slip.shape[1]
    cap = send_cells.shape[1] // n
    rest = cap - CAP_FAR
    peers = len(OFFSETS)
    total = cells + n * CAP_FAR + peers * rest
    dma = pltpu.SemaphoreType.DMA
    return pl.pallas_call(
        functools.partial(kernel, n, cells, cap),
        out_shape=jax.ShapeDtypeStruct(slip.shape, F32),
        in_specs=[pl.BlockSpec(memory_space=pltpu.VMEM)] * len(args),
        out_specs=pl.BlockSpec(memory_space=pltpu.VMEM),
        scratch_shapes=[
            pltpu.VMEM((n * cap, LANES), BF),
            pltpu.VMEM((n * CAP_FAR, LANES), BF),
            pltpu.VMEM((peers * rest, LANES), BF),
            pltpu.VMEM((2, HALO, LANES), BF),
            pltpu.VMEM((2 * HALO, LANES), BF),
            pltpu.VMEM((8, LANES), F32),
            pltpu.VMEM((n * 8, LANES), F32),
            pltpu.VMEM((6, LANES, LANES), F32),
            pltpu.VMEM((2 * LANES, 2 * LANES), BF),
            pltpu.VMEM((2, 2 * LANES, 2 * LANES), BF),
            pltpu.VMEM((2 * LANES, 2 * LANES), BF),
            pltpu.VMEM((2 * cells + 2 * n + 128, LANES), F32),
            pltpu.VMEM((cells + n + 128, 2 * LANES), F32),
            pltpu.VMEM((cells, LANES), F32),
            pltpu.VMEM((total // 256, round_up(far_list.shape[0], 8), cells), F32),
            pltpu.VMEM((2, round_up(near_list.shape[0], 8), cells), F32),
            pltpu.VMEM((LANES, total), BF),
            dma((n,)),
            dma((n,)),
            dma((peers,)),
            dma((peers,)),
            dma((2,)),
            dma((2,)),
            dma((n,)),
            dma((n,)),
        ],
        compiler_params=pltpu.CompilerParams(collective_id=0, has_side_effects=True),
    )(*args)


def solution(mesh):
    return jax.shard_map(
        body,
        mesh=mesh,
        in_specs=(
            P(None, "leaf"),
            P(),
            P(),
            P(),
            P(),
            P(),
            P(),
            P(),
            P("leaf", None),
            P(None, "leaf"),
            P(None, "leaf"),
        ),
        out_specs=P(None, "leaf"),
        check_vma=False,
    )
```

time: 93.6 us -> 43.5 us (0.46)
  Pallas kernels: 0 us -> 38.5 us
  local copies, waits for them, and re-layouts: 38 us -> 4.78 us
  starting transfers between devices: 24 us -> 0 us
  matrix products: 20.6 us -> 0 us
  waiting for transfers between devices: 5.89 us -> 0 us
  other arithmetic: 3.99 us -> 0 us
    pallas_call x0 -> x1, Pallas kernels: none -> 38.5 us  [body(): pl.pallas_call(functools.partial(kernel, n, cells, cap), out_shape=jax.Sh...]
    gather x3 -> x0, local copies, waits for them, and re-layouts: 31.5 us -> none  [the longest x1 14.7 us: body(): jnp.take(sources, far_list.reshape(-1), axis=1)]
    dot_general x67 -> x0, matrix products: 20.6 us -> none  [the longest x12 3.71 us: pair_up(): jnp.dot(up_shift[1], upper, precision=precise)]
    ppermute x7 -> x0, starting transfers between devices: 17.1 us -> none  [the longest x5 12.9 us: swapped(): return lax.ppermute(block, axis, route)]
    all_to_all x1 -> x0, starting transfers between devices: 6.95 us -> none  [body(): lax.all_to_all(outgoing, 'leaf', split_axis=1, concat_axis=1, tiled=True)]
    ppermute x7 -> x0, waiting for transfers between devices: 5.89 us -> none  [the longest x5 5.89 us: swapped(): return lax.ppermute(block, axis, route)]
    slice x17 -> x0, local copies, waits for them, and re-layouts: 5.15 us -> none  [the longest x14 2.66 us: body(): aggregates.append(pair_up(up_shift, below[:, 0::2], below[:, 1::2]))]
    unnamed x25 -> x8, local copies, waits for them, and re-layouts: 0.25 us -> 4.78 us
  transfers between devices with their start and end apart: 8 -> 0, of which waited for: 4 -> 0; matrix products, arithmetic and copies ran while one was open for 38% -> 0% of each run, Pallas kernels for 0% -> 0%
where the time goes in v1:
time: 43.5 us; the launch traced here: 43.3 us
  Pallas kernels  38.5 us (89%)
  local copies, waits for them, and re-layouts  4.78 us (11%)
    pallas_call x1, Pallas kernels, body(): pl.pallas_call(functools.partial(kernel, n, cells, cap), out_shape=jax.Sh...  38.5 us
    unnamed x8, local copies, waits for them, and re-layouts  4.78 us

profile of v1, /device:TPU:0, one launch (start us, length us, event | category | flops | bytes accessed | tf_op | source)
XLA Modules:
  0.0 43.3 jit_solution(12465282360194115718)
XLA Ops:
  0.0 0.0 copy-start
  0.0 1.6 %copy.12.up_ref = f32[2,121,121]{2,1,0:T(8,128)} copy(f32[2,121,121]{2,0,1:T(2,128)} %param.13) | data formatting | bytes 234256 | tf_op args[2]
  1.6 0.0 copy-done
  1.6 0.0 copy-start.1
  1.6 0.6 %copy.13.down_ref = f32[2,121,121]{2,1,0:T(8,128)} copy(f32[2,121,121]{2,0,1:T(2,128)S(1)} %copy-done) | data formatting | bytes 234256 | tf_op args[3]
  2.3 0.3 copy-done.1
  2.6 0.7 %copy.14.sib_ref = f32[2,121,121]{2,1,0:T(8,128)} copy(f32[2,121,121]{2,0,1:T(2,128)S(1)} %copy-done.1) | data formatting | bytes 234256 | tf_op args[4]
  3.2 38.5 %shard_map.109 = f32[128,256]{1,0:T(8,128)} custom-call(bf16[128,256]{1,0:T(8,128)(2,1)} %slip_ref.1, bf16[121,128]{1,0:T(8,128)(2,1)} %tm_ref.1, f32[2,121,121]{2,1,0:T(8,128)} %copy.12.up_ref, f32[2,121,121]{2,1,0:T(8,128)} %copy.13.down_ref, f32[2,121,121]{2,1,0:T(8,128)} %copy.14.sib_ref, bf16[27,121,121]{2,1,0:T(8,128)(2,1)} %leaf_ref.1, ...), custom_call_target="tpu_custom_call" | custom-call | tf_op jit(solution)/shard_map/pallas_call | solution.py:330
  41.7 1.6 %copy.16 = f32[128,256]{1,0:T(8,128)} copy(f32[128,256]{1,0:T(8,128)} %shard_map.109) | data formatting | bytes 262144
Async XLA Ops:
  0.0 1.6 %copy-start = (f32[2,121,121]{2,0,1:T(2,128)S(1)}, f32[2,121,121]{2,0,1:T(2,128)}, u32[]{:S(2)}) copy-start(f32[2,121,121]{2,0,1:T(2,128)} %param.14) | copy-start | bytes 351388
  1.6 0.9 %copy-start.1 = (f32[2,121,121]{2,0,1:T(2,128)S(1)}, f32[2,121,121]{2,0,1:T(2,128)}, u32[]{:S(2)}) copy-start(f32[2,121,121]{2,0,1:T(2,128)} %param.15) | copy-start | bytes 351388

commit v2 on v1

--- a/solution.py
+++ b/solution.py
@@ -38,7 +38,7 @@
     slip_ref, tm_ref, up_ref, down_ref, sib_ref, leaf_ref, ts_ref, nb_ref, send_ref, far_ref, near_ref,
     out_ref,
     outgoing, far_buf, near_buf, edges, halo, root_out, roots,
-    weight, w_up, w_sib, w_down, agg, terms, loc, rel, near_rel, source,
+    weight, w_up, w_sib, w_down, agg, terms, loc, rel, near_rel, source, leaf_cat, columns,
     far_send, far_recv, near_send, near_recv, halo_send, halo_recv, root_send, root_recv,
 ):
     me = lax.axis_index("leaf")
@@ -66,13 +66,6 @@
     weight[0, :coef, :] = tm_ref[...].astype(F32)
     multipole = mm(weight[0].astype(BF), slip_ref[...]).astype(BF)
     source[:, :cells] = multipole
-
-    chunk = 4 * cap
-    for start in range(0, n * cap, chunk):
-        picked = one_hot(cells, send_ref[0:1, start : start + chunk].astype(F32))
-        outgoing[start : start + chunk, :] = mm(multipole, picked).T.astype(BF)
-
-    pl.semaphore_wait(barrier, n - 1)
 
     def far_copy(k):
         target = lax.rem(me + k, n)
@@ -121,21 +114,6 @@
     def inside(offset):
         return jnp.logical_and(me + offset >= 0, me + offset < n)
 
-    for side in (0, 1):
-        @pl.when(inside(1 if side else -1))
-        def _():
-            halo_copy(side).start()
-
-    def start_far(k, carry):
-        far_copy(k).start()
-        return carry
-
-    lax.fori_loop(1, n, start_far, 0)
-    for j, offset in enumerate(OFFSETS):
-        @pl.when(inside(offset))
-        def _():
-            near_copy(j).start()
-
     def parts(ref, index):
         weight[index, :coef, :coef] = ref
         weight[index, :coef, coef:] = jnp.zeros((coef, LANES - coef), F32)
@@ -143,13 +121,13 @@
 
     w_sib[...] = jnp.zeros_like(w_sib)
     for s in (0, 1):
-        high, low = parts(up_ref[s], 0 + s)
+        high, low = parts(up_ref[:, s, :], 0 + s)
         w_up[s * LANES : (s + 1) * LANES, :LANES] = high
         w_up[s * LANES : (s + 1) * LANES, LANES:] = low
-        high, low = parts(down_ref[s], 2 + s)
+        high, low = parts(down_ref[:, s, :], 2 + s)
         w_down[:LANES, s * LANES : (s + 1) * LANES] = high
         w_down[LANES:, s * LANES : (s + 1) * LANES] = low
-        high, low = parts(sib_ref[s], 4 + s)
+        high, low = parts(sib_ref[:, s, :], 4 + s)
         other = 1 - s
         w_sib[0, other * LANES : (other + 1) * LANES, s * LANES : (s + 1) * LANES] = high
         w_sib[1, other * LANES : (other + 1) * LANES, s * LANES : (s + 1) * LANES] = low
@@ -193,11 +171,32 @@
     root_out[...] = value
     roots[pl.ds(pl.multiple_of(me * 8, 8), 8), :] = value
 
+    chunk = 4 * cap
+    for start in range(0, n * cap, chunk):
+        picked = one_hot(cells, send_ref[0:1, start : start + chunk].astype(F32))
+        outgoing[start : start + chunk, :] = mm(multipole, picked).T.astype(BF)
+
+    pl.semaphore_wait(barrier, n - 1)
+
     def start_root(k, carry):
         root_copy(k).start()
         return carry
 
     lax.fori_loop(1, n, start_root, 0)
+    for side in (0, 1):
+        @pl.when(inside(1 if side else -1))
+        def _():
+            halo_copy(side).start()
+
+    def start_far(k, carry):
+        far_copy(k).start()
+        return carry
+
+    lax.fori_loop(1, n, start_far, 0)
+    for j, offset in enumerate(OFFSETS):
+        @pl.when(inside(offset))
+        def _():
+            near_copy(j).start()
 
     v = far_ref[...]
     behind = v - cells
@@ -210,8 +209,8 @@
         v,
         jnp.where(
             slot < CAP_FAR,
-            cells + sender * CAP_FAR + slot,
-            cells + n * CAP_FAR + lane * rest + slot - CAP_FAR,
+            cells + near_buf.shape[0] + sender * CAP_FAR + slot,
+            cells + lane * rest + slot - CAP_FAR,
         ),
     )
     total = source.shape[1]
@@ -245,6 +244,41 @@
         stress = stress + mm(nb_ref[k], column.astype(BF))
     out_ref[...] = stress
 
+    leaf_cat[...] = jnp.zeros_like(leaf_cat)
+    for t in range(types):
+        leaf_cat[:coef, t * LANES : t * LANES + coef] = leaf_ref[t]
+
+    for j, offset in enumerate(OFFSETS):
+        @pl.when(inside(offset))
+        def _():
+            near_copy(j).wait_send()
+
+        @pl.when(inside(OFFSETS[len(OFFSETS) - 1 - j]))
+        def _():
+            near_copy(j).wait_recv()
+
+    close = cells + near_buf.shape[0]
+    source[:, cells:close] = near_buf[...].astype(F32).T.astype(BF)
+    group = 3 if types % 3 == 0 else 1
+
+    def gather(low, high, more):
+        def step(g, carry):
+            for i in range(group):
+                t = g * group + i
+                hits = jnp.concatenate(
+                    [one_hot(256, rel[b, pl.ds(t, 1), :]) for b in range(low, high)], axis=0
+                )
+                picked = mm(source[:, low * 256 : high * 256], hits).astype(BF)
+                rows = pl.ds(pl.multiple_of(t * LANES, LANES), LANES)
+                if more:
+                    picked = picked + columns[rows, :]
+                columns[rows, :] = picked
+            return carry
+
+        lax.fori_loop(0, types // group, step, 0)
+
+    gather(0, close // 256, False)
+
     def wait_root(k, carry):
         root_copy(k).wait()
         return carry
@@ -289,28 +323,10 @@
         return carry
 
     lax.fori_loop(1, n, wait_far, 0)
-    for j, offset in enumerate(OFFSETS):
-        @pl.when(inside(offset))
-        def _():
-            near_copy(j).wait_send()
-
-        @pl.when(inside(OFFSETS[len(OFFSETS) - 1 - j]))
-        def _():
-            near_copy(j).wait_recv()
-
-    far_end = cells + n * CAP_FAR
-    source[:, cells:far_end] = far_buf[...].astype(F32).T.astype(BF)
-    source[:, far_end:] = near_buf[...].astype(F32).T.astype(BF)
-
-    def leaf(t, acc):
-        hits = jnp.concatenate(
-            [one_hot(256, rel[b, pl.ds(t, 1), :]) for b in range(blocks)], axis=0
-        )
-        column = mm(source[...], hits).astype(BF)
-        return acc + mm(leaf_ref[t], column[:coef])
-
-    leaf_sum = lax.fori_loop(0, types, leaf, jnp.zeros((coef, cells), F32))
-    local_exp = (expansion.T[:coef] + leaf_sum).astype(BF)
+    source[:, close:] = far_buf[...].astype(F32).T.astype(BF)
+    gather(close // 256, blocks, True)
+    leaf_sum = mm(leaf_cat[...], columns[...])
+    local_exp = (expansion.T + leaf_sum)[:coef].astype(BF)
     out_ref[...] = out_ref[...] + mm(ts_ref[...], local_exp)
 
 
@@ -350,6 +366,8 @@
             pltpu.VMEM((total // 256, round_up(far_list.shape[0], 8), cells), F32),
             pltpu.VMEM((2, round_up(near_list.shape[0], 8), cells), F32),
             pltpu.VMEM((LANES, total), BF),
+            pltpu.VMEM((LANES, far_list.shape[0] * LANES), BF),
+            pltpu.VMEM((far_list.shape[0] * LANES, cells), BF),
             dma((n,)),
             dma((n,)),
             dma((peers,)),
@@ -360,7 +378,7 @@
             dma((n,)),
         ],
         compiler_params=pltpu.CompilerParams(collective_id=0, has_side_effects=True),
-    )(*args)
+    )(*(jnp.transpose(a, (1, 0, 2)) if 2 <= i < 5 else a for i, a in enumerate(args)))
 
 
 def solution(mesh):

time: 43.5 us -> 32.7 us (0.75)
  the two profiles are of different devices: /device:TPU:0 before, /device:TPU:15 now
where the time goes in v2:
time: 32.7 us; the launch traced here: 32.5 us
  Pallas kernels  31 us (95%)
  local copies, waits for them, and re-layouts  1.57 us (5%)
    pallas_call x1, Pallas kernels, body(): pl.pallas_call(functools.partial(kernel, n, cells, cap), out_shape=jax.Sh...  31 us
    unnamed x1, local copies, waits for them, and re-layouts  1.57 us

profile of v2, /device:TPU:15, one launch (start us, length us, event | category | flops | bytes accessed | tf_op | source)
XLA Modules:
  0.0 32.5 jit_solution(8705213181212928518)
XLA Ops:
  0.0 31.0 %shard_map.109 = f32[128,256]{1,0:T(8,128)} custom-call(bf16[128,256]{1,0:T(8,128)(2,1)} %slip_ref.1, bf16[121,128]{1,0:T(8,128)(2,1)} %tm_ref.1, f32[121,2,121]{2,1,0:T(2,128)} %bitcast.3, f32[121,2,121]{2,1,0:T(2,128)} %bitcast.4, f32[121,2,121]{2,1,0:T(2,128)} %bitcast.5, bf16[27,121,121]{2,1,0:T(8,128)(2,1)} %leaf_ref.1, bf16[128,121]{1,0:T(8,128)(2,1)} %ts_ref.1, ...), custom_call_target="tpu_custom_call" | custom-call | tf_op jit(solution)/shard_map/pallas_call | solution.py:346
  31.0 1.6 %copy.13 = f32[128,256]{1,0:T(8,128)} copy(f32[128,256]{1,0:T(8,128)} %shard_map.109) | data formatting | bytes 262144

commit v3 on v2

--- a/solution.py
+++ b/solution.py
@@ -35,10 +35,10 @@
 
 def kernel(
     n, cells, cap,
-    slip_ref, tm_ref, up_ref, down_ref, sib_ref, leaf_ref, ts_ref, nb_ref, send_ref, far_ref, near_ref,
+    slip_ref, tm_ref, up_ref, down_ref, sib_ref, leaf_any, ts_ref, nb_any, send_ref, far_ref, near_ref,
     out_ref,
     outgoing, far_buf, near_buf, edges, halo, root_out, roots,
-    weight, w_up, w_sib, w_down, agg, terms, loc, rel, near_rel, source, leaf_cat, columns,
+    weight, w_up, w_sib, w_down, agg, terms, loc, rel, near_rel, source, leaf_cat, columns, near_cols, leaf_ref, nb_ref, load_sem,
     far_send, far_recv, near_send, near_recv, halo_send, halo_recv, root_send, root_recv,
 ):
     me = lax.axis_index("leaf")
@@ -46,6 +46,13 @@
     types = far_ref.shape[0]
     kinds = near_ref.shape[0]
     rest = cap - CAP_FAR
+
+    loads = (
+        pltpu.make_async_copy(leaf_any, leaf_ref, load_sem.at[0]),
+        pltpu.make_async_copy(nb_any, nb_ref, load_sem.at[1]),
+    )
+    for copy in loads:
+        copy.start()
 
     barrier = pltpu.get_barrier_semaphore()
 
@@ -104,7 +111,7 @@
     def root_copy(k):
         return pltpu.make_async_remote_copy(
             src_ref=root_out,
-            dst_ref=roots.at[pl.ds(pl.multiple_of(me * 8, 8), 8)],
+            dst_ref=roots.at[me],
             send_sem=root_send.at[k],
             recv_sem=root_recv.at[k],
             device_id=(lax.rem(me + k, n),),
@@ -168,35 +175,13 @@
         value = lift(high, low)
         base += max(rows, 16)
         place(base, value)
-    root_out[...] = value
-    roots[pl.ds(pl.multiple_of(me * 8, 8), 8), :] = value
+    root_out[...] = value[:1]
+    roots[me] = value[:1]
 
     chunk = 4 * cap
     for start in range(0, n * cap, chunk):
         picked = one_hot(cells, send_ref[0:1, start : start + chunk].astype(F32))
         outgoing[start : start + chunk, :] = mm(multipole, picked).T.astype(BF)
-
-    pl.semaphore_wait(barrier, n - 1)
-
-    def start_root(k, carry):
-        root_copy(k).start()
-        return carry
-
-    lax.fori_loop(1, n, start_root, 0)
-    for side in (0, 1):
-        @pl.when(inside(1 if side else -1))
-        def _():
-            halo_copy(side).start()
-
-    def start_far(k, carry):
-        far_copy(k).start()
-        return carry
-
-    lax.fori_loop(1, n, start_far, 0)
-    for j, offset in enumerate(OFFSETS):
-        @pl.when(inside(offset))
-        def _():
-            near_copy(j).start()
 
     v = far_ref[...]
     behind = v - cells
@@ -218,47 +203,17 @@
     for b in range(blocks):
         rel[b, :types, :] = jnp.clip(position - 256 * b, -1, 256).astype(F32)
 
-    for side in (0, 1):
-        @pl.when(inside(1 if side else -1))
-        def _():
-            halo_copy(side).wait_send()
-
-        @pl.when(inside(-1 if side else 1))
-        def _():
-            halo_copy(side).wait_recv()
-
     w = near_ref[...]
     near_rel[0, :kinds, :] = jnp.clip(w - HALO, -1, cells).astype(F32)
     near_rel[1, :kinds, :] = jnp.where(
         w < HALO, w, jnp.where(w >= HALO + cells, w - cells, -1)
     ).astype(F32)
     slips = slip_ref[...]
-    side_slips = jnp.concatenate(
-        [halo[...], jnp.zeros((LANES - 2 * HALO, LANES), BF)], axis=0
-    ).astype(F32).T.astype(BF)
-    stress = jnp.zeros(out_ref.shape, F32)
     for k in range(kinds):
-        column = mm(slips, one_hot(cells, near_rel[0, k : k + 1, :])) + mm(
-            side_slips, one_hot(LANES, near_rel[1, k : k + 1, :])
-        )
-        stress = stress + mm(nb_ref[k], column.astype(BF))
-    out_ref[...] = stress
-
-    leaf_cat[...] = jnp.zeros_like(leaf_cat)
-    for t in range(types):
-        leaf_cat[:coef, t * LANES : t * LANES + coef] = leaf_ref[t]
-
-    for j, offset in enumerate(OFFSETS):
-        @pl.when(inside(offset))
-        def _():
-            near_copy(j).wait_send()
-
-        @pl.when(inside(OFFSETS[len(OFFSETS) - 1 - j]))
-        def _():
-            near_copy(j).wait_recv()
-
-    close = cells + near_buf.shape[0]
-    source[:, cells:close] = near_buf[...].astype(F32).T.astype(BF)
+        near_cols[k * LANES : (k + 1) * LANES, :] = mm(
+            slips, one_hot(cells, near_rel[0, k : k + 1, :])
+        ).astype(BF)
+
     group = 3 if types % 3 == 0 else 1
 
     def gather(low, high, more):
@@ -277,7 +232,68 @@
 
         lax.fori_loop(0, types // group, step, 0)
 
-    gather(0, close // 256, False)
+    gather(0, cells // 256, False)
+
+    for copy in loads:
+        copy.wait()
+    leaf_cat[...] = jnp.zeros_like(leaf_cat)
+    for t in range(types):
+        leaf_cat[:coef, t * LANES : t * LANES + coef] = leaf_ref[t]
+
+    pl.semaphore_wait(barrier, n - 1)
+
+    def start_root(k, carry):
+        root_copy(k).start()
+        return carry
+
+    lax.fori_loop(1, n, start_root, 0)
+    for side in (0, 1):
+        @pl.when(inside(1 if side else -1))
+        def _():
+            halo_copy(side).start()
+
+    for j, offset in enumerate(OFFSETS):
+        @pl.when(inside(offset))
+        def _():
+            near_copy(j).start()
+    def start_far(k, carry):
+        far_copy(lax.rem(k + n // 2 - 2, n - 1) + 1).start()
+        return carry
+
+    lax.fori_loop(1, n, start_far, 0)
+
+    for j, offset in enumerate(OFFSETS):
+        @pl.when(inside(offset))
+        def _():
+            near_copy(j).wait_send()
+
+        @pl.when(inside(OFFSETS[len(OFFSETS) - 1 - j]))
+        def _():
+            near_copy(j).wait_recv()
+
+    close = cells + near_buf.shape[0]
+    source[:, cells:close] = near_buf[...].astype(F32).T.astype(BF)
+    gather(cells // 256, close // 256, True)
+
+    for side in (0, 1):
+        @pl.when(inside(1 if side else -1))
+        def _():
+            halo_copy(side).wait_send()
+
+        @pl.when(inside(-1 if side else 1))
+        def _():
+            halo_copy(side).wait_recv()
+
+    side_slips = jnp.concatenate(
+        [halo[...], jnp.zeros((LANES - 2 * HALO, LANES), BF)], axis=0
+    ).astype(F32).T.astype(BF)
+    stress = jnp.zeros(out_ref.shape, F32)
+    for k in range(kinds):
+        column = near_cols[k * LANES : (k + 1) * LANES, :] + mm(
+            side_slips, one_hot(LANES, near_rel[1, k : k + 1, :])
+        ).astype(BF)
+        stress = stress + mm(nb_ref[k], column)
+    out_ref[...] = stress
 
     def wait_root(k, carry):
         root_copy(k).wait()
@@ -285,7 +301,7 @@
 
     lax.fori_loop(1, n, wait_root, 0)
     base = 0
-    place(base, roots[pl.ds(0, n, stride=8), :])
+    place(base, roots[:, 0, :])
     tree_spots = []
     for bit in range(tree_bits):
         rows = n >> bit
@@ -335,7 +351,7 @@
 
 
 def body(*args):
-    slip, to_multipole, _, _, _, _, _, _, send_cells, far_list, near_list = args
+    slip, _, _, _, _, leaf_far, _, near_blocks, send_cells, far_list, near_list = args
     n = lax.axis_size("leaf")
     cells = slip.shape[1]
     cap = send_cells.shape[1] // n
@@ -346,7 +362,9 @@
     return pl.pallas_call(
         functools.partial(kernel, n, cells, cap),
         out_shape=jax.ShapeDtypeStruct(slip.shape, F32),
-        in_specs=[pl.BlockSpec(memory_space=pltpu.VMEM)] * len(args),
+        in_specs=[
+            pl.BlockSpec(memory_space=pl.ANY if i in (5, 7) else pltpu.VMEM) for i in range(len(args))
+        ],
         out_specs=pl.BlockSpec(memory_space=pltpu.VMEM),
         scratch_shapes=[
             pltpu.VMEM((n * cap, LANES), BF),
@@ -354,8 +372,8 @@
             pltpu.VMEM((peers * rest, LANES), BF),
             pltpu.VMEM((2, HALO, LANES), BF),
             pltpu.VMEM((2 * HALO, LANES), BF),
-            pltpu.VMEM((8, LANES), F32),
-            pltpu.VMEM((n * 8, LANES), F32),
+            pltpu.VMEM((1, LANES), F32),
+            pltpu.VMEM((n, 1, LANES), F32),
             pltpu.VMEM((6, LANES, LANES), F32),
             pltpu.VMEM((2 * LANES, 2 * LANES), BF),
             pltpu.VMEM((2, 2 * LANES, 2 * LANES), BF),
@@ -368,6 +386,10 @@
             pltpu.VMEM((LANES, total), BF),
             pltpu.VMEM((LANES, far_list.shape[0] * LANES), BF),
             pltpu.VMEM((far_list.shape[0] * LANES, cells), BF),
+            pltpu.VMEM((near_list.shape[0] * LANES, cells), BF),
+            pltpu.VMEM(leaf_far.shape, BF),
+            pltpu.VMEM(near_blocks.shape, BF),
+            dma((2,)),
             dma((n,)),
             dma((n,)),
             dma((peers,)),

time: 32.7 us -> 28.4 us (0.87)
  the two profiles are of different devices: /device:TPU:15 before, /device:TPU:11 now
where the time goes in v3:
time: 28.4 us; the launch traced here: 28.2 us
  Pallas kernels  26.7 us (94%)
  local copies, waits for them, and re-layouts  1.57 us (6%)
    pallas_call x1, Pallas kernels, body(): pl.pallas_call(functools.partial(kernel, n, cells, cap), out_shape=jax.Sh...  26.7 us
    unnamed x1, local copies, waits for them, and re-layouts  1.57 us

profile of v3, /device:TPU:11, one launch (start us, length us, event | category | flops | bytes accessed | tf_op | source)
XLA Modules:
  0.0 28.2 jit_solution(3937349822182096116)
XLA Ops:
  0.0 26.7 %shard_map.109 = f32[128,256]{1,0:T(8,128)} custom-call(bf16[128,256]{1,0:T(8,128)(2,1)} %slip_ref.1, bf16[121,128]{1,0:T(8,128)(2,1)} %tm_ref.1, f32[121,2,121]{2,1,0:T(2,128)} %bitcast.3, f32[121,2,121]{2,1,0:T(2,128)} %bitcast.4, f32[121,2,121]{2,1,0:T(2,128)} %bitcast.5, bf16[27,121,121]{2,1,0:T(8,128)(2,1)} %leaf_any.1, bf16[128,121]{1,0:T(8,128)(2,1)} %ts_ref.1, ...), custom_call_target="tpu_custom_call" | custom-call | tf_op jit(solution)/shard_map/pallas_call | solution.py:362
  26.7 1.6 %copy.13 = f32[128,256]{1,0:T(8,128)} copy(f32[128,256]{1,0:T(8,128)} %shard_map.109) | data formatting | bytes 262144
